TPU v7x, 32 devices: a whole 2x2x4 slice. The times are simulated.
32 devices in a mesh: seq: 8 (over y, x, core), exp: 4 (over z).
Axes of the slice: x: 2, y: 2, z: 4, core: 2. Of those that a mesh axis runs over, the one named last changes fastest.
Arguments:
- grad_out: bfloat16 [4096, 2048], P(('seq', 'exp')), may hold values from -6 to 6
- out_proj: bfloat16 [4096, 2048], P('exp'), may hold values from -0.125 to 0.125
- step_size: float32 [64, 4096], P('exp', 'seq'), may hold values from 0.001 to 0.1
- log_decay: float32 [64, 4096], P('exp', 'seq'), may hold values from -1 to 0, as said below
- b_input: float32 [16, 4096], P(None, 'seq'), may hold values from -1.5 to 1.5
- c_output: float32 [16, 4096], P(None, 'seq'), may hold values from -1.5 to 1.5
- skip_gain: float32 [4096], P('exp'), may hold values from 0.5 to 1.5
- expert_ids: int32 [4096, 2], P('seq'), may hold values from 0 to 3, all different within a row; in each aligned block of 128 rows (0 to 127, 128 to 255, ...) at most 66 rows name the same one
- hidden_act: bfloat16 [4, 32, 66, 8192], P('exp', None, None, 'seq'), may hold values from -6 to 6
- w_down: bfloat16 [4, 8192, 2048], P('exp', 'seq'), may hold values from -0.0029296875 to 0.0029296875
Outputs:
- d_inner: bfloat16 [4096, 4096], P('seq', 'exp')
- d_gate: float32 [2, 4096], P(None, ('seq', 'exp'))
Inputs may be any that keep to these rules, and one draw needn't show every extreme that they name: `expert_ids`: each row names 2 different experts. Within the rows of one token group no expert is named by more than 66 rows, and in every draw some expert is named by exactly 66 rows of some group. `log_decay`: every entry is negative.
All inputs are finite; a program needn't handle non-finite values.
Results may differ from a plain program's by a relative error of at most 0.00065.
Values may be sent and summed in bfloat16 or wider, within the bound.
No kernel may reach another device: no remote copies, remote signals or barrier semaphores. Data moves between devices by JAX's collectives and lax.ppermute only.
A program may use at most 128 MiB of HBM per device.

v0:
```python
import jax
import jax.numpy as jnp
from jax import lax
from jax.sharding import PartitionSpec as P

HEAD = 64
highest = lax.Precision.HIGHEST


def block_pass(state_in, pieces):
    grad_block, decay_block, step_block, b_block, c_block = pieces
    cum_decay = jnp.cumsum(decay_block, axis=1)
    gap_table = cum_decay[:, None, :] - cum_decay[:, :, None]
    upper_mask = lax.broadcasted_iota(jnp.int32, gap_table.shape, 2) >= lax.broadcasted_iota(
        jnp.int32, gap_table.shape, 1
    )
    weights = jnp.where(upper_mask, jnp.exp(jnp.where(upper_mask, gap_table, 0.0)), 0.0)
    intersection = lax.dot_general(
        b_block,
        c_block,
        (((0,), (0,)), ((), ())),
        precision=highest,
        preferred_element_type=jnp.float32,
    )
    within = jnp.einsum("hut,thp->uhp", weights * intersection[None], grad_block, precision=highest)
    tail_decay = jnp.exp(cum_decay[:, -1:] - cum_decay)
    from_state = (
        jnp.einsum("nu,hnp->uhp", b_block, state_in, precision=highest) * tail_decay.T[:, :, None]
    )
    result = step_block.T[:, :, None] * (within + from_state)
    state_out = jnp.einsum(
        "ht,nt,thp->hnp", jnp.exp(cum_decay), c_block, grad_block, precision=highest
    )
    state_out = state_out + jnp.exp(cum_decay[:, -1])[:, None, None] * state_in
    return (state_out, result)


def local_sweep(grad_rows, decay_rows, step_rows, b_rows, c_rows, start_state):
    row_count = grad_rows.shape[0]
    head_count = decay_rows.shape[0]
    block_len = min(512, row_count)
    block_count = row_count // block_len
    pieces = (
        grad_rows.reshape(block_count, block_len, head_count, grad_rows.shape[2]),
        decay_rows.reshape(head_count, block_count, block_len).transpose(1, 0, 2),
        step_rows.reshape(head_count, block_count, block_len).transpose(1, 0, 2),
        b_rows.reshape(b_rows.shape[0], block_count, block_len).transpose(1, 0, 2),
        c_rows.reshape(c_rows.shape[0], block_count, block_len).transpose(1, 0, 2),
    )
    state_out, results = lax.scan(block_pass, start_state, pieces, reverse=True)
    return (state_out, results.reshape(row_count, head_count, grad_rows.shape[2]))


def route_table(groups, expert, cap_len):
    hit_mask = jnp.any(groups == expert, axis=2)
    rank_ids = jnp.cumsum(hit_mask.astype(jnp.int32), axis=1) - 1
    slot_ids = lax.broadcasted_iota(jnp.int32, (1, 1, cap_len), 2)
    chosen = jnp.logical_and(hit_mask[:, :, None], rank_ids[:, :, None] == slot_ids)
    token_ids = lax.broadcasted_iota(jnp.int32, chosen.shape, 1)
    position = jnp.sum(jnp.where(chosen, token_ids, 0), axis=1)
    filled = jnp.any(chosen, axis=1)
    return (position, filled)


def slot_lookup(slot_table, own_ids, cap_len, expert_count):
    experts_iota = lax.broadcasted_iota(jnp.int32, (1, 1, expert_count), 2)
    onehot = own_ids[:, :, None] == experts_iota
    member = jnp.any(onehot, axis=1).astype(jnp.int32)
    rank_ids = jnp.cumsum(member, axis=0) - 1
    slot_of = jnp.sum(jnp.where(onehot, rank_ids[:, None, :], 0), axis=2)
    picked = jnp.sum(jnp.where(onehot[:, :, :, None], slot_table[None, None], 0.0), axis=2)
    slot_iota = lax.broadcasted_iota(jnp.int32, (1, 1, cap_len), 2)
    return jnp.sum(jnp.where(slot_of[:, :, None] == slot_iota, picked, 0.0), axis=2)


def shards(
    grad_out,
    out_proj,
    step_size,
    log_decay,
    b_input,
    c_output,
    skip_gain,
    expert_ids,
    hidden_act,
    w_down,
):
    exp_index = lax.axis_index("exp")
    seq_index = lax.axis_index("seq")
    exp_count = lax.axis_size("exp")
    seq_count = lax.axis_size("seq")
    tok_len = grad_out.shape[0]
    cap_len = hidden_act.shape[2]
    gathered = lax.all_gather(grad_out, "exp", axis=0, tiled=True)
    groups = expert_ids.reshape(exp_count, tok_len, expert_ids.shape[1])
    position, filled = route_table(groups, exp_index, cap_len)
    flat_index = (position + lax.broadcasted_iota(jnp.int32, position.shape, 0) * tok_len).reshape(
        -1
    )
    slot_rows = jnp.take(gathered, flat_index, axis=0)
    slot_rows = jnp.where(filled.reshape(-1, 1), slot_rows, jnp.zeros_like(slot_rows))
    saved_rows = hidden_act.reshape(-1, hidden_act.shape[3])
    weights = w_down[0]
    projected = lax.dot_general(
        lax.all_gather(slot_rows, "seq", axis=0, tiled=True),
        weights,
        (((1,), (1,)), ((), ())),
        preferred_element_type=jnp.float32,
    )
    partial_scores = jnp.sum(projected * saved_rows.astype(jnp.float32), axis=1)
    head_count = out_proj.shape[0] // HEAD
    inner_grad = lax.dot_general(
        gathered, out_proj, (((1,), (1,)), ((), ())), preferred_element_type=jnp.float32
    )
    row_count = inner_grad.shape[0]
    start_state = jnp.zeros((head_count, b_input.shape[0], HEAD), jnp.float32)
    summary, swept_part = local_sweep(
        inner_grad.reshape(row_count, head_count, HEAD),
        log_decay,
        step_size,
        b_input,
        c_output,
        start_state,
    )
    total_decay = jnp.sum(log_decay, axis=1)
    all_states, all_decay = (
        lax.all_gather(summary[None], "seq", axis=0, tiled=True),
        lax.all_gather(total_decay[None], "seq", axis=0, tiled=True),
    )
    shard_ids = lax.broadcasted_iota(jnp.int32, all_decay.shape, 0)
    beyond = jnp.where(shard_ids > seq_index, all_decay, 0.0)
    exponent = jnp.cumsum(beyond, axis=0) - beyond
    factor = jnp.where(
        shard_ids > seq_index, jnp.exp(jnp.where(shard_ids > seq_index, exponent, 0.0)), 0.0
    )
    incoming = jnp.sum(factor[:, :, None, None] * all_states, axis=0)
    suffix = jnp.flip(jnp.cumsum(jnp.flip(log_decay, 1), axis=1), 1) - log_decay
    from_carry = (
        jnp.einsum("nu,hnp->uhp", b_input, incoming, precision=highest)
        * jnp.exp(suffix).T[:, :, None]
    )
    combined = swept_part + step_size.T[:, :, None] * from_carry
    d_inner = (combined.reshape(row_count, -1) + skip_gain * inner_grad).astype(jnp.bfloat16)
    summed = lax.psum_scatter(
        partial_scores.reshape(seq_count, exp_count, cap_len),
        "seq",
        scatter_dimension=0,
        tiled=True,
    )
    slot_table = lax.all_to_all(
        summed.reshape(exp_count, 1, cap_len), "exp", split_axis=0, concat_axis=1, tiled=True
    ).reshape(exp_count, cap_len)
    own_ids = lax.dynamic_slice_in_dim(expert_ids, exp_index * tok_len, tok_len, 0)
    d_gate = slot_lookup(slot_table, own_ids, cap_len, exp_count).T
    return (d_inner, d_gate)


def solution(mesh):
    in_specs = (
        P(("seq", "exp"), None),
        P("exp", None),
        P("exp", "seq"),
        P("exp", "seq"),
        P(None, "seq"),
        P(None, "seq"),
        P("exp"),
        P("seq", None),
        P("exp", None, None, "seq"),
        P("exp", "seq", None),
    )
    out_specs = (P("seq", "exp"), P(None, ("seq", "exp")))
    return jax.shard_map(shards, mesh=mesh, in_specs=in_specs, out_specs=out_specs, check_vma=False)
```

profile of v0, /device:TPU:0, one launch (start us, length us, event | category | flops | bytes accessed | tf_op | source)
XLA Modules:
  0.0 207.7 jit_solution(10610763480653563069)
XLA Ops:
  9.0 1.2 select_reduce_fusion.1
  10.5 1.2 fusion.21
  12.0 46.0 %all-gather.5.cloned.1.call-done = bf16[512,2048]{1,0:T(8,128)(2,1)} async-done(((bf16[128,2048]{1,0:T(8,128)(2,1)}), bf16[512,2048]{1,0:T(8,128)(2,1)}) %all-gather.5.cloned.1.call-update) | async-done | bytes 2097168 | tf_op jit(solution)/shard_map/all_gather | solution.py:94
  58.0 6.2 %gather_fusion = bf16[264,2048]{1,0:T(8,128)(2,1)S(1)} fusion(bf16[512,2048]{1,0:T(8,128)(2,1)} %all-gather.5.cloned.1.call-done, s32[1024]{0:T(1024)S(1)} %pad_clamp_fusion), kind=kCustom, calls=%fused_computation | custom fusion | bytes 2163744 | tf_op jit(solution)/shard_map/jit(_take)/gather | solution.py:100
  64.2 1.2 select_select_fusion
  67.1 1.2 reduce-window.16
  68.9 8.6 %copy.85 = f32[1,32,66,1024]{3,2,1,0:T(8,128)} copy(bf16[1,32,66,1024]{3,1,2,0:T(8,128)(2,1)} %param.18) | data formatting | bytes 12976128 | tf_op jit(solution)/shard_map/convert_element_type | solution.py:110
  77.5 9.5 %reshape.166 = f32[2112,1024]{1,0:T(8,128)} reshape(f32[1,32,66,1024]{3,2,1,0:T(8,128)} %copy.85) | data formatting | bytes 17301504 | tf_op jit(solution)/shard_map/convert_element_type | solution.py:110
  90.2 2.0 fusion.33
  92.2 3.1 %fusion.22 = f32[16,64,512]{2,1,0:T(8,128)} fusion(f32[16,512]{1,0:T(8,128)S(1)} %copy-done), kind=kOutput, calls=%fused_computation.34 | convolution fusion | flops 100663296 | bytes 2129920 | tf_op jit(solution)/shard_map/while/body/eval_jaxpr/nu,hnp->uhp/dot_general | solution.py:28
  95.3 5.9 %fusion.32 = f32[512,1024]{1,0:T(8,128)} fusion(bf16[512,2048]{1,0:T(8,128)(2,1)S(1)} %copy-done.1, bf16[1024,2048]{1,0:T(8,128)(2,1)} %param.11), kind=kOutput, calls=%fused_computation.74 | convolution fusion | flops 2147483648 | bytes 8388608 | tf_op jit(solution)/shard_map/dot_general | solution.py:112
  101.2 2.1 %copy.75 = f32[512,1024]{0,1:T(8,128)S(1)} copy(f32[512,1024]{1,0:T(8,128)} %fusion.32) | data formatting | bytes 4194304 | tf_op jit(solution)/shard_map/dot_general | solution.py:112
  103.3 1.8 convolution_add_fusion
  105.1 16.7 %all-gather.1 = f32[128,16,64]{2,1,0:T(8,128)S(1)} all-gather(f32[16,16,64]{2,1,0:T(8,128)S(1)} %convolution_add_fusion), channel_id=3, replica_groups=mesh['seq'=8,'exp'=4] {'seq'}, dimensions={0}, use_global_device_ids=true | all-gather | bytes 589824 | tf_op jit(solution)/shard_map/all_gather | solution.py:127
  121.7 2.2 %all-gather.7.cloned.1.call-done = bf16[2112,2048]{1,0:T(8,128)(2,1)} async-done(((bf16[264,2048]{1,0:T(8,128)(2,1)}), bf16[2112,2048]{1,0:T(8,128)(2,1)}) %all-gather.7.cloned.1.call-update) | async-done | bytes 8650768 | tf_op jit(solution)/shard_map/all_gather | solution.py:105
  123.9 14.9 %multiply_reduce_fusion = f32[2112]{0:T(1024)S(1)} fusion(f32[2112,1024]{1,0:T(8,128)} %reshape.166, bf16[2112,2048]{1,0:T(8,128)(2,1)} %all-gather.7.cloned.1.call-done, bf16[1,1024,2048]{2,1,0:T(8,128)(2,1)} %param.19), kind=kOutput, calls=%fused_computation.8 | convolution fusion | flops 8862693376 | bytes 21504256 | tf_op jit(solution)/shard_map/dot_general | solution.py:104
  139.0 23.5 %all-reduce.2 = (f32[128]{0:T(128)S(1)}, f32[8,4,66]{2,1,0:T(4,128)S(1)}) all-reduce(f32[128]{0:T(128)S(1)} %dynamic-update-slice, f32[8,4,66]{2,1,0:T(4,128)S(1)} %reshape.164), channel_id=2, replica_groups=mesh['seq'=8,'exp'=4] {'seq'}, use_global_device_ids=true, to_apply=%add | all-reduce | flops 2240 | bytes 17920
  163.0 1.8 fusion.24
  164.8 20.5 %fusion.12 = f32[512,16,64]{0,2,1:T(8,128)} fusion(f32[16,64,512]{2,1,0:T(8,128)S(1)} %fusion.24, f32[16,64,512]{2,1,0:T(8,128)S(1)} %copy-done.3, f32[512,16,64]{0,2,1:T(8,128)S(1)} %bitcast.79, f32[512,512]{1,0:T(8,128)S(1)} %copy-done.4, f32[16,512]{1,0:T(8,128)S(1)} %copy_bitcast_fusion.1, f32[512,16]{0,1:T(8,128)S(1)} %get-tuple-element.22, ...), kind=kOutput, calls=%fused_computation.16 | convolution fusion | flops 3244818432 | bytes 9568256 | tf_op jit(solution)/shard_map/while/body/eval_jaxpr/hut,thp->uhp/dot_general | solution.py:25
  185.4 3.0 %copy.80 = f32[512,1024]{1,0:T(8,128)} copy(f32[512,1024]{0,1:T(8,128)} %bitcast.81) | data formatting | bytes 4194304 | tf_op jit(solution)/shard_map/reshape | solution.py:143
  188.4 1.2 constant_dynamic-slice_fusion
  189.6 4.7 %all-to-all-start = ((f32[4,1,66]{2,1,0:T(1,128)}), f32[4,1,66]{2,1,0:T(1,128)S(1)}, u32[]{:S(2)}, u32[]{:S(2)}) async-start(f32[4,1,66]{2,1,0:T(1,128)} %bitcast.17), calls=%async_computation | async-start | bytes 4096 | tf_op jit(solution)/shard_map/all_to_all | solution.py:150
  194.3 3.1 %add_convert_fusion = bf16[512,1024]{1,0:T(8,128)(2,1)} fusion(f32[512,1024]{1,0:T(8,128)} %copy.80, f32[512,1024]{1,0:T(8,128)S(1)} %copy-done.2, f32[1024]{0:T(1024)S(1)} %copy-done.7), kind=kLoop, calls=%fused_computation.19 | loop fusion | flops 1572864 | bytes 5246976 | tf_op jit(solution)/shard_map/convert_element_type | solution.py:143
  197.4 2.5 %all-to-all-done = f32[4,1,66]{2,1,0:T(1,128)S(1)} async-done(((f32[4,1,66]{2,1,0:T(1,128)}), f32[4,1,66]{2,1,0:T(1,128)S(1)}, u32[]{:S(2)}, u32[]{:S(2)}) %all-to-all-start) | async-done | bytes 1088 | tf_op jit(solution)/shard_map/all_to_all | solution.py:150
  (76 shorter events, 8.7 us)
Async XLA Ops:
  7.2 83.1 %copy-start = (f32[16,512]{1,0:T(8,128)S(1)}, f32[16,512]{1,0:T(8,128)}, u32[]{:S(2)}) copy-start(f32[16,512]{1,0:T(8,128)} %param.14) | copy-start | bytes 98308
  7.2 50.8 %all-gather.5.cloned.1.call-start = ((), (), s32[]{:S(2)}) async-start(), calls=%async_computation.1 | async-start | bytes 2621440 | tf_op jit(solution)/shard_map/all_gather | solution.py:94
  7.9 116.0 %all-gather.7.cloned.1.call-start = ((), (), s32[]{:S(2)}) async-start(), calls=%async_computation.2 | async-start | bytes 9732096 | tf_op jit(solution)/shard_map/all_gather | solution.py:105
  64.2 1.3 copy-start.5
  77.5 10.7 %copy-start.8 = (u32[32]{0:T(128)S(1)}, u32[32]{0:T(128)}, u32[]{:S(2)}) copy-start(u32[32]{0:T(128)} %constant.76) | copy-start | bytes 388
  77.5 12.8 %copy-start.6 = (f32[16,512]{1,0:T(8,128)S(1)}, f32[16,512]{1,0:T(8,128)}, u32[]{:S(2)}) copy-start(f32[16,512]{1,0:T(8,128)} %param.15) | copy-start | bytes 98308
  87.0 8.3 %copy-start.1 = (bf16[512,2048]{1,0:T(8,128)(2,1)S(1)}, bf16[512,2048]{1,0:T(8,128)(2,1)}, u32[]{:S(2)}) copy-start(bf16[512,2048]{1,0:T(8,128)(2,1)} %all-gather.5.cloned.1.call-done) | copy-start | bytes 6291460
  138.9 25.9 %copy-start.9 = (f32[16,512]{1,0:T(8,128)S(1)}, f32[16,512]{1,0:T(8,128)}, u32[]{:S(2)}) copy-start(f32[16,512]{1,0:T(8,128)} %param.12) | copy-start | bytes 98308
  162.7 2.2 %copy-start.3 = (f32[16,64,512]{2,1,0:T(8,128)S(1)}, f32[16,64,512]{2,1,0:T(8,128)}, u32[]{:S(2)}) copy-start(f32[16,64,512]{2,1,0:T(8,128)} %fusion.22) | copy-start | bytes 6291460
  162.7 2.2 %copy-start.4 = (f32[512,512]{1,0:T(8,128)S(1)}, f32[512,512]{1,0:T(8,128)}, u32[]{:S(2)}) copy-start(f32[512,512]{1,0:T(8,128)} %fusion.33) | copy-start | bytes 3145732
  185.4 9.0 %copy-start.2 = (f32[512,1024]{1,0:T(8,128)S(1)}, f32[512,1024]{1,0:T(8,128)}, u32[]{:S(2)}) copy-start(f32[512,1024]{1,0:T(8,128)} %fusion.32) | copy-start | bytes 6291460
  185.4 9.0 %copy-start.7 = (f32[1024]{0:T(1024)S(1)}, f32[1024]{0:T(1024)}, u32[]{:S(2)}) copy-start(f32[1024]{0:T(1024)} %param.16) | copy-start | bytes 12292
  189.6 10.3 %all-to-all-start = ((f32[4,1,66]{2,1,0:T(1,128)}), f32[4,1,66]{2,1,0:T(1,128)S(1)}, u32[]{:S(2)}, u32[]{:S(2)}) async-start(f32[4,1,66]{2,1,0:T(1,128)} %bitcast.17), calls=%async_computation | async-start | bytes 4096 | tf_op jit(solution)/shard_map/all_to_all | solution.py:150
Sparse Core Ops, SparseCore 0:
  9.6 48.3 all-gather.4
  65.6 58.3 all-gather.6
where the time goes:
time: 208 us
  waiting for transfers between devices  51.4 us (25%)
  matrix products  50 us (24%)
  blocking collectives  40.1 us (19%)
  local copies, waits for them, and re-layouts  34.5 us (17%)
  between operations  14.9 us (7%)
  other arithmetic  12 us (6%)
  starting transfers between devices  4.76 us (2%)
    all_gather x1, waiting for transfers between devices, shards(): gathered = lax.all_gather(grad_out, 'exp', axis=0, tiled=True)  46 us
    unnamed x1, blocking collectives  23.5 us
    dot_general x1, matrix products, block_pass(): jnp.einsum('hut,thp->uhp', weights * intersection[None], grad_block, prec...  20.5 us
    convert_element_type x2, local copies, waits for them, and re-layouts, shards(): partial_scores = jnp.sum(projected * saved_rows.astype(jnp.float32), axis=1)  18.1 us
    all_gather x1, blocking collectives, shards(): lax.all_gather(summary[None], 'seq', axis=0, tiled=True)  16.7 us
    dot_general x1, matrix products, shards(): lax.dot_general(lax.all_gather(slot_rows, 'seq', axis=0, tiled=True), wei...  14.9 us
    gather x1, local copies, waits for them, and re-layouts, shards(): slot_rows = jnp.take(gathered, flat_index, axis=0)  6.22 us
    dot_general x1, matrix products, shards(): lax.dot_general(gathered, out_proj, (((1,), (1,)), ((), ())), preferred_e...  5.91 us
  transfers between devices with their start and end apart: 3, of which 3 were waited for; matrix products, arithmetic and copies ran while one was open for 22% of the time, Pallas kernels for 0%

commit v1 on v0

--- a/solution.py
+++ b/solution.py
@@ -91,7 +91,12 @@
     seq_count = lax.axis_size("seq")
     tok_len = grad_out.shape[0]
     cap_len = hidden_act.shape[2]
-    gathered = lax.all_gather(grad_out, "exp", axis=0, tiled=True)
+    ring = [grad_out]
+    for hop in range(3):
+        ring.append(lax.ppermute(ring[-1], "exp", [(dev, (dev + 1) % 4) for dev in range(4)]))
+    gathered = jnp.roll(
+        jnp.concatenate(ring[::-1], axis=0), (lax.axis_index("exp") + 1) * ring[0].shape[0], axis=0
+    )
     groups = expert_ids.reshape(exp_count, tok_len, expert_ids.shape[1])
     position, filled = route_table(groups, exp_index, cap_len)
     flat_index = (position + lax.broadcasted_iota(jnp.int32, position.shape, 0) * tok_len).reshape(

time: 208 us -> 202 us (0.971)
  waiting for transfers between devices: 51.4 us -> 43.3 us
  starting transfers between devices: 4.76 us -> 7.74 us
    all_gather x1 -> x0, waiting for transfers between devices: 46 us -> none  [shards(): gathered = lax.all_gather(grad_out, 'exp', axis=0, tiled=True)]
    ppermute x0 -> x3, waiting for transfers between devices: none -> 39.1 us  [shards(): lax.ppermute(ring[-1], 'exp', [(dev, (dev + 1) % 4) for dev in range(4)])]
    gather x1, local copies, waits for them, and re-layouts: 6.22 us -> 2.6 us  [shards(): slot_rows = jnp.take(gathered, flat_index, axis=0)]
    ppermute x0 -> x3, starting transfers between devices: none -> 3.11 us  [shards(): lax.ppermute(ring[-1], 'exp', [(dev, (dev + 1) % 4) for dev in range(4)])]
  transfers between devices with their start and end apart: 3 -> 5, of which waited for: 3 -> 5; matrix products, arithmetic and copies ran while one was open for 22% -> 23% of each run, Pallas kernels for 0% -> 0%
where the time goes in v1:
time: 202 us; the launch traced here: 201 us
  matrix products  51.1 us (25%)
  waiting for transfers between devices  43.3 us (21%)
  blocking collectives  39.7 us (20%)
  local copies, waits for them, and re-layouts  32.5 us (16%)
  between operations  14.9 us (7%)
  other arithmetic  12 us (6%)
  starting transfers between devices  7.74 us (4%)
    ppermute x3, waiting for transfers between devices, shards(): lax.ppermute(ring[-1], 'exp', [(dev, (dev + 1) % 4) for dev in range(4)])  39.1 us
    unnamed x1, blocking collectives  23.5 us
    dot_general x1, matrix products, block_pass(): jnp.einsum('hut,thp->uhp', weights * intersection[None], grad_block, prec...  21.6 us
    convert_element_type x2, local copies, waits for them, and re-layouts, shards(): partial_scores = jnp.sum(projected * saved_rows.astype(jnp.float32), axis=1)  18.5 us
    all_gather x1, blocking collectives, shards(): lax.all_gather(summary[None], 'seq', axis=0, tiled=True)  16.2 us
    dot_general x1, matrix products, shards(): lax.dot_general(lax.all_gather(slot_rows, 'seq', axis=0, tiled=True), wei...  14.9 us
    dot_general x1, matrix products, shards(): lax.dot_general(gathered, out_proj, (((1,), (1,)), ((), ())), preferred_e...  5.9 us
    all_to_all x1, starting transfers between devices, shards(): lax.all_to_all(summed.reshape(exp_count, 1, cap_len), 'exp', split_axis=0...  4.6 us
  transfers between devices with their start and end apart: 5, of which 5 were waited for; matrix products, arithmetic and copies ran while one was open for 23% of the time, Pallas kernels for 0%

profile of v1, /device:TPU:0, one launch (start us, length us, event | category | flops | bytes accessed | tf_op | source)
XLA Modules:
  0.0 201.2 jit_solution(15751425900371117789)
XLA Ops:
  7.2 3.1 %collective-permute-start = (bf16[128,2048]{1,0:T(8,128)(2,1)}, bf16[128,2048]{1,0:T(8,128)(2,1)S(1)}, u32[]{:S(2)}, u32[]{:S(2)}) collective-permute-start(bf16[128,2048]{1,0:T(8,128)(2,1)} %param.10), channel_id=1, source_target_pairs={{0,1},{1,2},{2,3},{3,0},{4,5},{5,6},{6,7},{7,4},{8,9},{9,10},{10,1... | collective-permute-start | bytes 1572872 | tf_op jit(solution)/shard_map/ppermute | solution.py:96
  11.4 13.1 %collective-permute-done = bf16[128,2048]{1,0:T(8,128)(2,1)S(1)} collective-permute-done((bf16[128,2048]{1,0:T(8,128)(2,1)}, bf16[128,2048]{1,0:T(8,128)(2,1)S(1)}, u32[]{:S(2)}, u32[]{:S(2)}) %collective-permute-start) | collective-permute-done | bytes 524320 | tf_op jit(solution)/shard_map/ppermute | solution.py:96
  26.0 13.4 %collective-permute-done.1 = bf16[128,2048]{1,0:T(8,128)(2,1)S(1)} collective-permute-done((bf16[128,2048]{1,0:T(8,128)(2,1)S(1)}, bf16[128,2048]{1,0:T(8,128)(2,1)S(1)}, u32[]{:S(2)}, u32[]{:S(2)}) %collective-permute-start.1) | collective-permute-done | bytes 524320 | tf_op jit(solution)/shard_map/ppermute | solution.py:96
  40.8 12.6 %collective-permute-done.2 = bf16[128,2048]{1,0:T(8,128)(2,1)S(1)} collective-permute-done((bf16[128,2048]{1,0:T(8,128)(2,1)S(1)}, bf16[128,2048]{1,0:T(8,128)(2,1)S(1)}, u32[]{:S(2)}, u32[]{:S(2)}) %collective-permute-start.2) | collective-permute-done | bytes 524320 | tf_op jit(solution)/shard_map/ppermute | solution.py:96
  55.0 2.6 %gather_fusion = bf16[264,2048]{1,0:T(8,128)(2,1)S(1)} fusion(bf16[512,2048]{1,0:T(8,128)(2,1)S(1)} %constant_dynamic-slice_fusion.2, s32[1024]{0:T(1024)S(1)} %pad_clamp_fusion), kind=kCustom, calls=%fused_computation | custom fusion | bytes 2163744 | tf_op jit(solution)/shard_map/jit(_take)/gather | solution.py:105
  57.6 1.2 select_select_fusion
  62.3 9.0 %copy.85 = f32[1,32,66,1024]{3,2,1,0:T(8,128)} copy(bf16[1,32,66,1024]{3,1,2,0:T(8,128)(2,1)} %param.18) | data formatting | bytes 12976128 | tf_op jit(solution)/shard_map/convert_element_type | solution.py:115
  71.3 9.5 %reshape.166 = f32[2112,1024]{1,0:T(8,128)} reshape(f32[1,32,66,1024]{3,2,1,0:T(8,128)} %copy.85) | data formatting | bytes 17301504 | tf_op jit(solution)/shard_map/convert_element_type | solution.py:115
  83.9 2.0 fusion.33
  85.9 3.1 %fusion.22 = f32[16,64,512]{2,1,0:T(8,128)} fusion(f32[16,512]{1,0:T(8,128)S(1)} %copy-done), kind=kOutput, calls=%fused_computation.34 | convolution fusion | flops 100663296 | bytes 2129920 | tf_op jit(solution)/shard_map/while/body/eval_jaxpr/nu,hnp->uhp/dot_general | solution.py:28
  89.0 5.9 %fusion.32 = f32[512,1024]{1,0:T(8,128)} fusion(bf16[512,2048]{1,0:T(8,128)(2,1)S(1)} %constant_dynamic-slice_fusion.2, bf16[1024,2048]{1,0:T(8,128)(2,1)} %param.11), kind=kOutput, calls=%fused_computation.83 | convolution fusion | flops 2147483648 | bytes 8388608 | tf_op jit(solution)/shard_map/dot_general | solution.py:117
  94.9 1.9 copy.75
  96.8 1.8 convolution_add_fusion
  98.5 16.2 %all-gather.1 = f32[128,16,64]{2,1,0:T(8,128)S(1)} all-gather(f32[16,16,64]{2,1,0:T(8,128)S(1)} %convolution_add_fusion), channel_id=3, replica_groups=mesh['seq'=8,'exp'=4] {'seq'}, dimensions={0}, use_global_device_ids=true | all-gather | bytes 589824 | tf_op jit(solution)/shard_map/all_gather | solution.py:132
  114.8 1.7 all-gather.4.cloned.1.call-done
  116.5 14.9 %multiply_reduce_fusion = f32[2112]{0:T(1024)S(1)} fusion(f32[2112,1024]{1,0:T(8,128)} %reshape.166, bf16[2112,2048]{1,0:T(8,128)(2,1)} %all-gather.4.cloned.1.call-done, bf16[1,1024,2048]{2,1,0:T(8,128)(2,1)} %param.19), kind=kOutput, calls=%fused_computation.8 | convolution fusion | flops 8862693376 | bytes 21504256 | tf_op jit(solution)/shard_map/dot_general | solution.py:109
  131.5 23.5 %all-reduce.2 = (f32[128]{0:T(128)S(1)}, f32[8,4,66]{2,1,0:T(4,128)S(1)}) all-reduce(f32[128]{0:T(128)S(1)} %dynamic-update-slice, f32[8,4,66]{2,1,0:T(4,128)S(1)} %reshape.164), channel_id=2, replica_groups=mesh['seq'=8,'exp'=4] {'seq'}, use_global_device_ids=true, to_apply=%add | all-reduce | flops 2240 | bytes 17920
  155.5 1.8 fusion.24
  157.3 21.6 %fusion.12 = f32[512,16,64]{0,2,1:T(8,128)} fusion(f32[16,64,512]{2,1,0:T(8,128)S(1)} %fusion.24, f32[16,64,512]{2,1,0:T(8,128)} %fusion.22, f32[512,16,64]{0,2,1:T(8,128)S(1)} %bitcast.79, f32[512,512]{1,0:T(8,128)} %fusion.33, f32[16,512]{1,0:T(8,128)S(1)} %copy_bitcast_fusion.1, f32[512,16]{0,1:T(8,128)S(1)} %get-tuple-element.22, ...), kind=kOutput, calls=%fused_computation.16 | convolution fusion | flops 3244818432 | bytes 9568256 | tf_op jit(solution)/shard_map/while/body/eval_jaxpr/hut,thp->uhp/dot_general | solution.py:25
  178.9 3.1 %copy.80 = f32[512,1024]{1,0:T(8,128)} copy(f32[512,1024]{0,1:T(8,128)} %bitcast.81) | data formatting | bytes 4194304 | tf_op jit(solution)/shard_map/reshape | solution.py:148
  182.0 1.2 constant_dynamic-slice_fusion
  183.2 4.6 %all-to-all-start = ((f32[4,1,66]{2,1,0:T(1,128)}), f32[4,1,66]{2,1,0:T(1,128)S(1)}, u32[]{:S(2)}, u32[]{:S(2)}) async-start(f32[4,1,66]{2,1,0:T(1,128)} %bitcast.17), calls=%async_computation | async-start | bytes 4096 | tf_op jit(solution)/shard_map/all_to_all | solution.py:155
  187.8 3.1 %add_convert_fusion = bf16[512,1024]{1,0:T(8,128)(2,1)} fusion(f32[512,1024]{1,0:T(8,128)} %copy.80, f32[512,1024]{1,0:T(8,128)S(1)} %copy-done.1, f32[1024]{0:T(1024)S(1)} %copy-done.5), kind=kLoop, calls=%fused_computation.19 | loop fusion | flops 1572864 | bytes 5246976 | tf_op jit(solution)/shard_map/convert_element_type | solution.py:148
  190.9 2.5 %all-to-all-done = f32[4,1,66]{2,1,0:T(1,128)S(1)} async-done(((f32[4,1,66]{2,1,0:T(1,128)}), f32[4,1,66]{2,1,0:T(1,128)S(1)}, u32[]{:S(2)}, u32[]{:S(2)}) %all-to-all-start) | async-done | bytes 1088 | tf_op jit(solution)/shard_map/all_to_all | solution.py:155
  (84 shorter events, 12.9 us)
Async XLA Ops:
  7.2 76.7 %copy-start = (f32[16,512]{1,0:T(8,128)S(1)}, f32[16,512]{1,0:T(8,128)}, u32[]{:S(2)}) copy-start(f32[16,512]{1,0:T(8,128)} %param.14) | copy-start | bytes 98308
  7.2 47.6 %copy-start.2 = (bf16[128,2048]{1,0:T(8,128)(2,1)S(1)}, bf16[128,2048]{1,0:T(8,128)(2,1)}, u32[]{:S(2)}) copy-start(bf16[128,2048]{1,0:T(8,128)(2,1)} %param.10) | copy-start | bytes 1572868
  7.2 109.3 %all-gather.4.cloned.1.call-start = ((), (), s32[]{:S(2)}) async-start(), calls=%async_computation.1 | async-start | bytes 9732096 | tf_op jit(solution)/shard_map/all_gather | solution.py:110
  7.2 17.3 %collective-permute-start = (bf16[128,2048]{1,0:T(8,128)(2,1)}, bf16[128,2048]{1,0:T(8,128)(2,1)S(1)}, u32[]{:S(2)}, u32[]{:S(2)}) collective-permute-start(bf16[128,2048]{1,0:T(8,128)(2,1)} %param.10), channel_id=1, source_target_pairs={{0,1},{1,2},{2,3},{3,0},{4,5},{5,6},{6,7},{7,4},{8,9},{9,10},{10,1... | collective-permute-start | bytes 1572872 | tf_op jit(solution)/shard_map/ppermute | solution.py:96
  24.5 14.9 %collective-permute-start.1 = (bf16[128,2048]{1,0:T(8,128)(2,1)S(1)}, bf16[128,2048]{1,0:T(8,128)(2,1)S(1)}, u32[]{:S(2)}, u32[]{:S(2)}) collective-permute-start(bf16[128,2048]{1,0:T(8,128)(2,1)S(1)} %collective-permute-done), channel_id=1, source_target_pairs={{0,1},{1,2},{2,3},{3,0},{4,5},{5,6},{6,7},{7,4},{8,9},{9,10},{10,1... | collective-permute-start | bytes 1572872 | tf_op jit(solution)/shard_map/ppermute | solution.py:96
  39.4 14.0 %collective-permute-start.2 = (bf16[128,2048]{1,0:T(8,128)(2,1)S(1)}, bf16[128,2048]{1,0:T(8,128)(2,1)S(1)}, u32[]{:S(2)}, u32[]{:S(2)}) collective-permute-start(bf16[128,2048]{1,0:T(8,128)(2,1)S(1)} %collective-permute-done.1), channel_id=1, source_target_pairs={{0,1},{1,2},{2,3},{3,0},{4,5},{5,6},{6,7},{7,4},{8,9},{9,10},{10,1... | collective-permute-start | bytes 1572872 | tf_op jit(solution)/shard_map/ppermute | solution.py:96
  55.0 3.9 %copy-start.3 = (f32[16,512]{1,0:T(8,128)S(1)}, f32[16,512]{1,0:T(8,128)}, u32[]{:S(2)}) copy-start(f32[16,512]{1,0:T(8,128)} %param.13) | copy-start | bytes 98308
  71.3 10.6 %copy-start.6 = (u32[32]{0:T(128)S(1)}, u32[32]{0:T(128)}, u32[]{:S(2)}) copy-start(u32[32]{0:T(128)} %constant.97) | copy-start | bytes 388
  71.3 12.6 %copy-start.4 = (f32[16,512]{1,0:T(8,128)S(1)}, f32[16,512]{1,0:T(8,128)}, u32[]{:S(2)}) copy-start(f32[16,512]{1,0:T(8,128)} %param.15) | copy-start | bytes 98308
  114.8 42.5 %copy-start.7 = (f32[16,512]{1,0:T(8,128)S(1)}, f32[16,512]{1,0:T(8,128)}, u32[]{:S(2)}) copy-start(f32[16,512]{1,0:T(8,128)} %param.12) | copy-start | bytes 98308
  178.9 8.9 %copy-start.1 = (f32[512,1024]{1,0:T(8,128)S(1)}, f32[512,1024]{1,0:T(8,128)}, u32[]{:S(2)}) copy-start(f32[512,1024]{1,0:T(8,128)} %fusion.32) | copy-start | bytes 6291460
  178.9 8.9 %copy-start.5 = (f32[1024]{0:T(1024)S(1)}, f32[1024]{0:T(1024)}, u32[]{:S(2)}) copy-start(f32[1024]{0:T(1024)} %param.16) | copy-start | bytes 12292
  183.2 10.2 %all-to-all-start = ((f32[4,1,66]{2,1,0:T(1,128)}), f32[4,1,66]{2,1,0:T(1,128)S(1)}, u32[]{:S(2)}, u32[]{:S(2)}) async-start(f32[4,1,66]{2,1,0:T(1,128)} %bitcast.17), calls=%async_computation | async-start | bytes 4096 | tf_op jit(solution)/shard_map/all_to_all | solution.py:155
Sparse Core Ops, SparseCore 0:
  59.0 57.4 all-gather.3
